TPU v7x, 32 devices: a whole 2x2x4 slice. The times are simulated.
32 devices in a mesh: seq: 8 (over z, y), grp: 4 (over x, core).
Axes of the slice: x: 2, y: 2, z: 4, core: 2. Of those that a mesh axis runs over, the one named last changes fastest.
Arguments:
- doc_lengths: int32 [4, 4], P('grp'), may hold values from 1 to 512, 1024 in all within a row
- hidden: bfloat16 [4, 1024, 7168], P('grp', 'seq'), may hold values from -6 to 6
- gate_weight: bfloat16 [7168, 64], P(('seq', 'grp')), may hold values from -0.0625 to 0.0625
- target_query: bfloat16 [4, 1024, 36864], P('grp', 'seq'), may hold values from -30 to 30
- latent_keys: bfloat16 [4, 1024, 576], P('grp', 'seq'), may hold values from -6 to 6
- index_query: bfloat16 [4, 1024, 8192], P('grp', 'seq'), may hold values from -15 to 15
- index_keys: bfloat16 [4, 1024, 128], P('grp', 'seq'), may hold values from -6 to 6
Outputs:
- divergence: float32 [4, 1024], P('grp', 'seq')
- grad_gate: float32 [7168, 64], P(('seq', 'grp'))
All inputs are finite; a program needn't handle non-finite values.
Results may differ from a plain program's by a relative error of at most 0.0022.
Values may be sent and summed in bfloat16 or wider, within the bound.
No kernel may reach another device: no remote copies, remote signals or barrier semaphores. Data moves between devices by JAX's collectives and lax.ppermute only.
A program may use at most 128 MiB of HBM per device.

v0:
```python
import jax
import jax.numpy as jnp
from jax import lax
from jax.sharding import PartitionSpec as P

LOOK = 8


target_scale = 0.07216878364870322
highest = lax.Precision.HIGHEST
floor_value = -1e30


def shifted(block, axis, distance):
    devices = range(lax.axis_size(axis))
    route = [(i - distance, i) for i in devices if i - distance in devices]
    return lax.ppermute(block, axis, route)


def piece_terms(
    target_rows,
    index_rows,
    gate_rows,
    latent_panel,
    index_panel,
    panel_start_offset,
    positions,
    lengths,
    doc_most,
):
    piece_count, piece_rows = positions.shape
    latent_width = latent_panel.shape[1]
    index_width = index_panel.shape[1]
    key_tile = 128
    span_keys = (doc_most + piece_rows - 1 + key_tile - 1) // key_tile * key_tile
    doc_ends = jnp.cumsum(lengths)
    starts = jnp.sum(lengths * (doc_ends <= positions[..., None]).astype(jnp.int32), -1)
    tile_counts = (positions[:, -1] + 1 - starts[:, 0] + key_tile - 1) // key_tile
    ranking = jnp.argsort(tile_counts, stable=True)
    batch_pieces = max(1, 16 // piece_rows)
    batch_count = piece_count // batch_pieces
    factor = index_width ** (-0.5)
    latent_padded = jnp.concatenate(
        [latent_panel, jnp.zeros((key_tile, latent_width), latent_panel.dtype)], 0
    )
    index_padded = jnp.concatenate(
        [index_panel, jnp.zeros((key_tile, index_width), index_panel.dtype)], 0
    )
    offsets = jnp.arange(key_tile, dtype=jnp.int32)

    def one_batch(batch_index):
        chosen = lax.dynamic_slice_in_dim(ranking, batch_index * batch_pieces, batch_pieces, 0)
        queries = jnp.take(target_rows, chosen, axis=0).reshape(
            batch_pieces, piece_rows, -1, latent_width
        )
        indexer_query_rows = jnp.take(index_rows, chosen, axis=0).reshape(
            batch_pieces, piece_rows, -1, index_width
        )
        gate_values = jnp.take(gate_rows, chosen, axis=0)
        row_pos = jnp.take(positions, chosen, axis=0)
        row_start = jnp.take(starts, chosen, axis=0)
        anchor = row_start[:, 0]
        turn_count = jnp.max(jnp.take(tile_counts, chosen, axis=0))
        head_count = queries.shape[2]
        gate_heads = gate_values.shape[2]

        def allowed_of(turn_index):
            key_pos = anchor[:, None] + turn_index * key_tile + offsets[None, :]
            return (key_pos[:, None, :] >= row_start[:, :, None]) & (
                key_pos[:, None, :] <= row_pos[:, :, None]
            )

        def cut_panel(first_key):
            return (
                lax.dynamic_slice_in_dim(
                    latent_padded, first_key - panel_start_offset, key_tile, 0
                ),
                lax.dynamic_slice_in_dim(index_padded, first_key - panel_start_offset, key_tile, 0),
            )

        def first_pass(turn_index, carry):
            logit_store, relu_store, head_peak, head_total, score_peak, score_total = carry
            latent_tile, indexer_key_block = jax.vmap(cut_panel)(anchor + turn_index * key_tile)
            allowed = allowed_of(turn_index)
            logits = (
                jnp.einsum(
                    "brhc,bkc->brhk", queries, latent_tile, preferred_element_type=jnp.float32
                )
                * target_scale
            )
            relu_score = jnp.maximum(
                jnp.einsum(
                    "fjme,fve->fjmv",
                    indexer_query_rows,
                    indexer_key_block,
                    preferred_element_type=jnp.float32,
                ),
                0.0,
            )
            score = factor * jnp.einsum("brh,brhk->brk", gate_values, relu_score, precision=highest)
            masked = jnp.where(allowed[:, :, None, :], logits, floor_value)
            new_peak = jnp.maximum(head_peak, jnp.max(masked, -1))
            head_total = head_total * jnp.exp(head_peak - new_peak) + jnp.sum(
                jnp.where(allowed[:, :, None, :], jnp.exp(masked - new_peak[..., None]), 0.0), -1
            )
            masked_score = jnp.where(allowed, score, floor_value)
            new_score_peak = jnp.maximum(score_peak, jnp.max(masked_score, -1))
            score_total = score_total * jnp.exp(score_peak - new_score_peak) + jnp.sum(
                jnp.where(allowed, jnp.exp(masked_score - new_score_peak[..., None]), 0.0), -1
            )
            logit_store = lax.dynamic_update_slice_in_dim(
                logit_store, logits, turn_index * key_tile, 3
            )
            relu_store = lax.dynamic_update_slice_in_dim(
                relu_store, relu_score, turn_index * key_tile, 3
            )
            return (logit_store, relu_store, new_peak, head_total, new_score_peak, score_total)

        start_carry = (
            jnp.zeros((batch_pieces, piece_rows, head_count, span_keys), jnp.float32),
            jnp.zeros((batch_pieces, piece_rows, gate_heads, span_keys), jnp.float32),
            jnp.full((batch_pieces, piece_rows, head_count), floor_value, jnp.float32),
            jnp.zeros((batch_pieces, piece_rows, head_count), jnp.float32),
            jnp.full((batch_pieces, piece_rows), floor_value, jnp.float32),
            jnp.zeros((batch_pieces, piece_rows), jnp.float32),
        )
        logit_store, relu_store, head_peak, head_total, score_peak, score_total = lax.fori_loop(
            0, turn_count, first_pass, start_carry
        )
        head_log = head_peak + jnp.log(head_total)
        score_log = score_peak + jnp.log(score_total)

        def second_pass(turn_index, carry):
            row_div, delta_terms = carry
            allowed = allowed_of(turn_index)
            logits = lax.dynamic_slice_in_dim(logit_store, turn_index * key_tile, key_tile, 3)
            relu_score = lax.dynamic_slice_in_dim(relu_store, turn_index * key_tile, key_tile, 3)
            probabilities = jnp.where(
                allowed[:, :, None, :], jnp.exp(logits - head_log[..., None]), 0.0
            )
            target = jnp.mean(probabilities, axis=2)
            score = factor * jnp.einsum("brh,brhk->brk", gate_values, relu_score, precision=highest)
            log_model = jnp.where(allowed, score - score_log[..., None], 0.0)
            model_prob = jnp.where(allowed, jnp.exp(log_model), 0.0)
            positive = target > 0
            target_log_probabilities = jnp.where(
                positive, target * jnp.log(jnp.where(positive, target, 1.0)), 0.0
            )
            row_div = row_div + jnp.sum(
                jnp.where(allowed, target_log_probabilities - target * log_model, 0.0), -1
            )
            delta_terms = delta_terms + factor * jnp.einsum(
                "brk,brhk->brh", model_prob - target, relu_score, precision=highest
            )
            return (row_div, delta_terms)

        return lax.fori_loop(
            0,
            turn_count,
            second_pass,
            (
                jnp.zeros((batch_pieces, piece_rows), jnp.float32),
                jnp.zeros((batch_pieces, piece_rows, gate_heads), jnp.float32),
            ),
        )

    sorted_div, sorted_delta = lax.map(one_batch, jnp.arange(batch_count, dtype=jnp.int32))
    sorted_div = sorted_div.reshape(piece_count, piece_rows)
    sorted_delta = sorted_delta.reshape(piece_count, piece_rows, -1)
    row_div = jnp.zeros_like(sorted_div).at[ranking].set(sorted_div)
    delta_terms = jnp.zeros_like(sorted_delta).at[ranking].set(sorted_delta)
    return (row_div, delta_terms)


def body(doc_lengths, hidden, gate_weight, target_query, latent_keys, index_query, index_keys):
    seq_count = lax.axis_size("seq")
    my_index = lax.axis_index("seq")
    row_count = hidden.shape[1]
    reach_devices = min(LOOK, seq_count // 2)
    doc_most = reach_devices * row_count
    lengths = doc_lengths[0]
    full_gate = lax.all_gather(gate_weight, ("seq", "grp"), axis=0, tiled=True)
    block_rows = 16
    block_count = row_count // block_rows
    latent_parts = []
    index_parts = []
    for offset in range(reach_devices, 0, -1):
        latent_prev, index_prev = shifted((latent_keys[0], index_keys[0]), "seq", offset)
        latent_parts.append(latent_prev)
        index_parts.append(index_prev)
    latent_win = jnp.concatenate(latent_parts + [latent_keys[0]], 0)
    index_win = jnp.concatenate(index_parts + [index_keys[0]], 0)
    panel_start_offset = my_index * row_count - doc_most
    positions = (my_index * row_count + jnp.arange(row_count, dtype=jnp.int32)).reshape(
        block_count, block_rows
    )
    gates_home = jnp.dot(hidden[0], full_gate, preferred_element_type=jnp.float32).reshape(
        block_count, block_rows, -1
    )
    row_div, delta_terms = piece_terms(
        target_query[0].reshape(block_count, block_rows, -1),
        index_query[0].reshape(block_count, block_rows, -1),
        gates_home,
        latent_win,
        index_win,
        panel_start_offset,
        positions,
        lengths,
        doc_most,
    )
    gate_delta = (delta_terms.reshape(row_count, -1) / row_count).astype(jnp.bfloat16)
    partial_value = jnp.dot(hidden[0].T, gate_delta, preferred_element_type=jnp.float32)
    divergence = row_div.reshape(1, row_count)
    grad_gate = lax.psum_scatter(partial_value, ("seq", "grp"), scatter_dimension=0, tiled=True)
    return (divergence, grad_gate)


def solution(mesh):
    in_specs = (
        P("grp", None),
        P("grp", "seq", None),
        P(("seq", "grp"), None),
        P("grp", "seq", None),
        P("grp", "seq", None),
        P("grp", "seq", None),
        P("grp", "seq", None),
    )
    out_specs = (P("grp", "seq"), P(("seq", "grp"), None))
    return jax.shard_map(body, mesh=mesh, in_specs=in_specs, out_specs=out_specs, check_vma=False)
```

profile of v0, /device:TPU:0, one launch (start us, length us, event | category | flops | bytes accessed | tf_op | source)
XLA Modules:
  0.0 749.1 jit_solution(18029676043556172486)
XLA Ops:
  7.2 6.8 collective-permute-start
  14.0 4.4 collective-permute-start.1
  19.8 3.1 collective-permute-start.3
  25.9 40.9 %all-gather = bf16[32,224,64]{1,2,0:T(8,128)(2,1)S(1)} all-gather(bf16[1,224,64]{1,2,0:T(8,128)(2,1)} %bitcast.275), channel_id=1, replica_groups=mesh['seq'=8,'grp'=4] {'seq','grp'}, dimensions={0}, use_global_device_ids=true | all-gather | bytes 946176 | tf_op jit(solution)/shard_map/all_gather | solution.py:182
  68.5 2.6 reshape.572
  78.5 6.3 collective-permute-start.7
  93.3 227.2 %while.59 = (s32[]{:T(128)}, f32[8,1,16]{2,1,0:T(1,128)S(1)}, f32[8,1,16,64]{3,2,1,0:T(8,128)}, s32[8]{0:T(128)S(1)}, s32[8]{0:T(128)S(1)}, /*index=5*/s32[8]{0:...) while((s32[]{:T(128)}, f32[8,1,16]{2,1,0:T(1,128)S(1)}, ...), condition=%wide.region_14.16_spmd.clone.clone, body=%wide.region_3.15_spmd.clone.clone.sunk | while | flops 191511280 | bytes 18097928 | solution.py:167
  98.8 2.4 dynamic-slice_select_fusion.5
  101.2 2.7 select_n.240
  109.8 6.1 while.60
  112.7 2.4 bitcast_dynamic-update-slice_fusion.7
  115.9 5.2 while.61
  119.1 2.0 fusion.67
  127.2 2.4 dynamic-slice_select_fusion.5
  129.6 2.7 select_n.240
  138.2 6.1 while.60
  138.2 1.9 bitcast_dynamic-update-slice_fusion.8
  141.1 2.4 bitcast_dynamic-update-slice_fusion.7
  144.3 5.2 while.61
  147.5 2.0 fusion.67
  155.6 2.4 dynamic-slice_select_fusion.5
  158.0 2.7 select_n.240
  166.6 6.1 while.60
  166.6 1.8 bitcast_dynamic-update-slice_fusion.8
  169.5 2.4 bitcast_dynamic-update-slice_fusion.7
  172.7 5.2 while.61
  175.9 2.0 fusion.67
  184.0 2.4 dynamic-slice_select_fusion.5
  186.4 2.7 select_n.240
  195.0 6.1 while.60
  195.0 1.9 bitcast_dynamic-update-slice_fusion.8
  197.9 2.4 bitcast_dynamic-update-slice_fusion.7
  201.1 5.2 while.61
  204.3 2.0 fusion.67
  212.4 2.4 dynamic-slice_select_fusion.5
  214.8 2.7 select_n.240
  223.4 6.1 while.60
  223.4 1.8 bitcast_dynamic-update-slice_fusion.8
  226.3 2.4 bitcast_dynamic-update-slice_fusion.7
  229.5 5.2 while.61
  232.7 2.0 fusion.67
  240.8 2.4 dynamic-slice_select_fusion.5
  243.2 2.7 select_n.240
  251.8 6.1 while.60
  251.8 1.9 bitcast_dynamic-update-slice_fusion.8
  254.7 2.4 bitcast_dynamic-update-slice_fusion.7
  257.9 5.2 while.61
  261.1 2.0 fusion.67
  269.2 2.4 dynamic-slice_select_fusion.5
  271.6 2.7 select_n.240
  280.2 6.1 while.60
  280.2 1.8 bitcast_dynamic-update-slice_fusion.8
  283.1 2.4 bitcast_dynamic-update-slice_fusion.7
  286.3 5.2 while.61
  289.5 2.0 fusion.67
  297.6 2.4 dynamic-slice_select_fusion.5
  300.0 2.7 select_n.240
  308.6 6.1 while.60
  308.6 1.9 bitcast_dynamic-update-slice_fusion.8
  311.5 2.4 bitcast_dynamic-update-slice_fusion.7
  314.7 5.2 while.61
  317.9 2.0 fusion.67
  323.6 3.5 copy.19
  328.4 412.3 %reduce-scatter.4.cloned.1.call-done = f32[224,64]{1,0:T(8,128)} async-done(((f32[7168,64]{1,0:T(8,128)}), f32[224,64]{1,0:T(8,128)}) %reduce-scatter.4.cloned.1.call-update) | async-done | bytes 57360
  (381 shorter events, 125.8 us)
Async XLA Ops:
  7.2 64.9 %copy-start = (bf16[1,128,7168]{2,1,0:T(8,128)(2,1)S(1)}, bf16[1,128,7168]{2,1,0:T(8,128)(2,1)}, u32[]{:S(2)}) copy-start(bf16[1,128,7168]{2,1,0:T(8,128)(2,1)} %param.16) | copy-start | bytes 5505028
  7.2 733.5 %reduce-scatter.4.cloned.1.call-start = ((), (), s32[]{:S(2)}) async-start(), calls=%async_computation.1 | async-start | bytes 3784704
  7.2 81.0 %collective-permute-start = (bf16[128,576]{0,1:T(8,128)(2,1)}, bf16[128,576]{0,1:T(8,128)(2,1)}, u32[]{:S(2)}, u32[]{:S(2)}) collective-permute-start(bf16[128,576]{0,1:T(8,128)(2,1)} %bitcast.269), channel_id=1, source_target_pairs={{0,16},{4,20},{8,24},{12,28},{1,17},{5,21},{9,25},{13,29},{2,18},{... | collective-permute-start | bytes 442376 | tf_op jit(solution)/shard_map/ppermute | solution.py:17
  14.0 75.8 %collective-permute-start.1 = (bf16[128,576]{0,1:T(8,128)(2,1)}, bf16[128,576]{0,1:T(8,128)(2,1)S(1)}, u32[]{:S(2)}, u32[]{:S(2)}) collective-permute-start(bf16[128,576]{0,1:T(8,128)(2,1)} %bitcast.270), channel_id=1, source_target_pairs={{0,12},{4,16},{8,20},{12,24},{16,28},{1,13},{5,17},{9,21},{13,25},... | collective-permute-start | bytes 442376 | tf_op jit(solution)/shard_map/ppermute | solution.py:17
  18.4 72.0 %collective-permute-start.2 = (bf16[128,576]{0,1:T(8,128)(2,1)}, bf16[128,576]{0,1:T(8,128)(2,1)S(1)}, u32[]{:S(2)}, u32[]{:S(2)}) collective-permute-start(bf16[128,576]{0,1:T(8,128)(2,1)} %bitcast.271), channel_id=1, source_target_pairs={{0,8},{4,12},{8,16},{12,20},{16,24},{20,28},{1,9},{5,13},{9,17},{1... | collective-permute-start | bytes 442376 | tf_op jit(solution)/shard_map/ppermute | solution.py:17
  19.8 71.4 %collective-permute-start.3 = (bf16[128,576]{0,1:T(8,128)(2,1)}, bf16[128,576]{0,1:T(8,128)(2,1)S(1)}, u32[]{:S(2)}, u32[]{:S(2)}) collective-permute-start(bf16[128,576]{0,1:T(8,128)(2,1)} %bitcast.272), channel_id=1, source_target_pairs={{0,4},{4,8},{8,12},{12,16},{16,20},{20,24},{24,28},{1,5},{5,9},{9,... | collective-permute-start | bytes 442376 | tf_op jit(solution)/shard_map/ppermute | solution.py:17
  22.9 49.9 %collective-permute-start.4 = (bf16[128,128]{1,0:T(8,128)(2,1)}, bf16[128,128]{1,0:T(8,128)(2,1)S(1)}, u32[]{:S(2)}, u32[]{:S(2)}) collective-permute-start(bf16[128,128]{1,0:T(8,128)(2,1)} %bitcast.276), channel_id=1, source_target_pairs={{0,16},{4,20},{8,24},{12,28},{1,17},{5,21},{9,25},{13,29},{2,18},{... | collective-permute-start | bytes 98312 | tf_op jit(solution)/shard_map/ppermute | solution.py:17
  68.5 4.3 copy-start.2
  71.1 20.8 %copy-start.1 = (bf16[1,128,576]{1,2,0:T(8,128)(2,1)S(1)}, bf16[1,128,576]{1,2,0:T(8,128)(2,1)}, u32[]{:S(2)}) copy-start(bf16[1,128,576]{1,2,0:T(8,128)(2,1)} %param.19) | copy-start | bytes 442372
  72.7 2.9 collective-permute-start.5
  75.6 2.9 collective-permute-start.6
  78.5 7.9 %collective-permute-start.7 = (bf16[128,128]{1,0:T(8,128)(2,1)S(1)}, bf16[128,128]{1,0:T(8,128)(2,1)S(1)}, u32[]{:S(2)}, u32[]{:S(2)}) collective-permute-start(bf16[128,128]{1,0:T(8,128)(2,1)S(1)} %bitcast.279), channel_id=1, source_target_pairs={{0,4},{4,8},{8,12},{12,16},{16,20},{20,24},{24,28},{1,5},{5,9},{9,... | collective-permute-start | bytes 98312 | tf_op jit(solution)/shard_map/ppermute | solution.py:17
Sparse Core Ops, SparseCore 0:
  327.3 413.3 reduce-scatter.3
where the time goes:
time: 758 us; the launch traced here: 749 us
  waiting for transfers between devices  415 us (55%)
  local copies, waits for them, and re-layouts  91.4 us (12%)
  matrix products  69 us (9%)
  other arithmetic  51.3 us (7%)
  loops' own time  41.2 us (5%)
  blocking collectives  40.9 us (5%)
  starting transfers between devices  25.8 us (3%)
  between operations  14.2 us (2%)
    unnamed x2, waiting for transfers between devices  412 us
    all_gather x1, blocking collectives, body(): full_gate = lax.all_gather(gate_weight, ('seq', 'grp'), axis=0, tiled=True)  40.9 us
    another operation x1, loops' own time, piece_terms(): lax.map(one_batch, jnp.arange(batch_count, dtype=jnp.int32))  39.1 us
    another operation x64, local copies, waits for them, and re-layouts  28.8 us
    ppermute x8, starting transfers between devices, shifted(): return lax.ppermute(block, axis, route)  25.8 us
    select_n x8, local copies, waits for them, and re-layouts, one_batch(): jnp.take(target_rows, chosen, axis=0)  21.2 us
    select_n x8, other arithmetic, one_batch(): jnp.take(target_rows, chosen, axis=0)  19.2 us
    dot_general x8, matrix products, first_pass(): jnp.einsum('brhc,bkc->brhk', queries, latent_tile, preferred_element_type...  19 us
  transfers between devices with their start and end apart: 9, of which 4 were waited for; matrix products, arithmetic and copies ran while one was open for 2% of the time, Pallas kernels for 0%

commit v1 on v0

v1 whole, which is shorter than its diff:
```python
import functools
import math
import jax
import jax.numpy as jnp
from jax import lax
from jax.experimental import pallas as pl
from jax.experimental.pallas import tpu as pltpu
from jax.sharding import PartitionSpec as P

LOOK = 8
LANES = 128
CHUNK = 64

target_scale = 0.07216878364870322
log2e = 1.4426950408889634
floor_value = -1e30
NT = (((1,), (1,)), ((), ()))
TN = (((0,), (0,)), ((), ()))


def shifted(block, axis, distance):
    devices = range(lax.axis_size(axis))
    route = [(i - distance, i) for i in devices if i - distance in devices]
    return lax.ppermute(block, axis, route)


def bit_steps():
    steps = []
    for axis in ("seq", "grp"):
        size = lax.axis_size(axis)
        bit = size // 2
        while bit:
            steps.append((axis, bit))
            bit //= 2
    return steps


def swap(block, axis, bit):
    return lax.ppermute(block, axis, [(i, i ^ bit) for i in range(lax.axis_size(axis))])


def bit_of(axis, bit):
    return (lax.axis_index(axis) // bit) % 2


def reversed_bits(number, width):
    result = 0
    for _ in range(width):
        result = result * 2 + number % 2
        number //= 2
    return result


def row_window(lens_ref, first_row, panel_start, keys, rows):
    position = first_row + lax.broadcasted_iota(jnp.int32, (1, rows), 1)
    start = jnp.zeros((1, rows), jnp.int32)
    end = jnp.int32(0)
    for d in range(lens_ref.shape[0]):
        length = lens_ref[d]
        end = end + length
        start = start + jnp.where(position >= end, length, 0)

    def allowed(low, count):
        key = panel_start + low + lax.broadcasted_iota(jnp.int32, (count, rows), 0)
        return (key >= start) & (key <= position)

    return allowed


def fold8(value):
    return value.reshape(value.shape[0] // 8, 8, value.shape[1])


def target_kernel(reach, lens_ref, idx_ref, *refs):
    lat_refs = refs[: reach + 1]
    q_hbm, out_ref, q_v, ke, ko, sa, sb, bias, sem = refs[reach + 1 :]
    block = pl.program_id(0)
    rows = out_ref.shape[1]
    keys = out_ref.shape[0]
    width = lat_refs[0].shape[1]
    device_rows = lat_refs[0].shape[0]
    slab = ke.shape[1]
    pair = 2 * width
    pads = slab - width
    heads = q_v.shape[1] // width
    loops = heads // 4
    parts = sem.shape[0]
    part_cols = q_v.shape[1] // parts
    loops_per_part = loops // parts

    def part_copy(i):
        cols = pl.ds(pl.multiple_of(i * part_cols, LANES), part_cols)
        return pltpu.make_async_copy(
            q_hbm.at[pl.ds(pl.multiple_of(block * rows, rows), rows), cols], q_v.at[:, cols], sem.at[i]
        )

    for i in range(parts):
        part_copy(i).start()

    @pl.when(block == 0)
    def _():
        for i, lat in enumerate(lat_refs):
            spot = pl.ds(i * device_rows, device_rows)
            values = lat[...].astype(jnp.float32)
            wide = jnp.concatenate([values, jnp.zeros((device_rows, pads), jnp.float32)], 1)
            ke[spot, :] = wide.astype(jnp.bfloat16)
            ko[spot, :] = pltpu.roll(wide, pads, 1).astype(jnp.bfloat16)

    first_row = idx_ref[0] * device_rows + block * rows
    panel_start = (idx_ref[0] - reach) * device_rows
    allowed = row_window(lens_ref, first_row, panel_start, keys, rows)
    for low in range(0, keys, CHUNK):
        bias[pl.ds(low, CHUNK), :] = jnp.where(allowed(low, CHUNK), 0.0, floor_value)
        out_ref[pl.ds(low, CHUNK), :] = jnp.zeros((CHUNK, rows), jnp.float32)

    def logits(j, shift, panel, store):
        base = j * (2 * pair) + shift
        q0 = q_v[:, pl.ds(pl.multiple_of(base, LANES), slab)]
        q1 = q_v[:, pl.ds(pl.multiple_of(base + pair, LANES), slab)]
        both = jnp.concatenate([q0, q1], 0)
        value = lax.dot_general(panel[...], both, NT, preferred_element_type=jnp.float32)
        peak = jnp.full((8, 2 * rows), floor_value, jnp.float32)
        for low in range(0, keys, CHUNK):
            piece_bias = bias[pl.ds(low, CHUNK), :]
            piece = value[low : low + CHUNK] + jnp.concatenate([piece_bias, piece_bias], 1)
            store[pl.ds(low, CHUNK), :] = piece
            peak = jnp.maximum(peak, jnp.max(fold8(piece), 0))
        return jnp.max(peak, 0, keepdims=True)

    def softmax_add(store, peak):
        total = jnp.zeros((8, 2 * rows), jnp.float32)
        for low in range(0, keys, CHUNK):
            piece = jnp.exp2((store[pl.ds(low, CHUNK), :] - peak) * (target_scale * log2e))
            store[pl.ds(low, CHUNK), :] = piece
            total = total + jnp.sum(fold8(piece), 0)
        scale = 1.0 / (jnp.sum(total, 0, keepdims=True) * heads)
        for low in range(0, keys, CHUNK):
            piece = store[pl.ds(low, CHUNK), :] * scale
            out_ref[pl.ds(low, CHUNK), :] += piece[:, :rows] + piece[:, rows:]

    part_copy(0).wait()
    peak_a = logits(0, 0, ke, sa)

    def step(j, peak_a):
        peak_b = logits(j, pair - slab, ko, sb)
        softmax_add(sa, peak_a)
        after = jnp.minimum(j + 1, loops - 1)

        @pl.when((after % loops_per_part == 0) & (after > j))
        def _():
            part_copy(after // loops_per_part).wait()

        peak_a = logits(after, 0, ke, sa)
        softmax_add(sb, peak_b)
        return peak_a

    lax.fori_loop(0, loops, step, peak_a)


def target_call(lengths, index, lat_parts, queries):
    reach = len(lat_parts) - 1
    rows_all, cols = queries.shape
    width = lat_parts[0].shape[1]
    rows = LANES
    keys = (reach + 1) * rows_all
    slab = (width + LANES - 1) // LANES * LANES
    parts = 8
    return pl.pallas_call(
        functools.partial(target_kernel, reach),
        out_shape=jax.ShapeDtypeStruct((keys, rows_all), jnp.float32),
        grid_spec=pltpu.PrefetchScalarGridSpec(
            num_scalar_prefetch=2,
            grid=(rows_all // rows,),
            in_specs=[pl.BlockSpec((rows_all, width), lambda i, *_: (0, 0))] * (reach + 1)
            + [pl.BlockSpec(memory_space=pl.ANY)],
            out_specs=pl.BlockSpec((keys, rows), lambda i, *_: (0, i)),
            scratch_shapes=[
                pltpu.VMEM((rows, cols), jnp.bfloat16),
                pltpu.VMEM((keys, slab), jnp.bfloat16),
                pltpu.VMEM((keys, slab), jnp.bfloat16),
                pltpu.VMEM((keys, 2 * rows), jnp.float32),
                pltpu.VMEM((keys, 2 * rows), jnp.float32),
                pltpu.VMEM((keys, rows), jnp.float32),
                pltpu.SemaphoreType.DMA((parts,)),
            ],
        ),
        compiler_params=pltpu.CompilerParams(dimension_semantics=("arbitrary",)),
        cost_estimate=pl.CostEstimate(
            flops=2 * rows_all * cols * keys,
            bytes_accessed=rows_all * cols * 2,
            transcendentals=rows_all * cols // width * keys,
        ),
        name="target_terms",
    )(lengths, index, *lat_parts, queries)


def index_kernel(reach, bits, lens_ref, idx_ref, *refs):
    key_refs = refs[: reach + 1]
    (target_ref, hidden_ref, weight_ref, query_ref, div_ref, part_ref, panel, weight, gates, score, delta) = refs[
        reach + 1 :
    ]
    block = pl.program_id(0)
    keys, rows = target_ref.shape
    device_rows, width = key_refs[0].shape
    heads = query_ref.shape[1] // width
    blocks, block_rows, _ = weight_ref.shape
    half = blocks * block_rows
    factor = width ** (-0.5)
    unroll = 4

    @pl.when(block == 0)
    def _():
        for i, ref in enumerate(key_refs):
            panel[pl.ds(i * device_rows, device_rows), :] = ref[...]
        for i in range(blocks):
            weight[pl.ds(reversed_bits(i, bits) * block_rows, block_rows), :] = weight_ref[i]

    low_gates = jnp.dot(hidden_ref[:, :half], weight[...], preferred_element_type=jnp.float32)
    high_gates = jnp.dot(hidden_ref[:, half:], weight[...], preferred_element_type=jnp.float32)
    gates[...] = low_gates[:, :heads].T + high_gates[:, heads:].T
    for low in range(0, keys, CHUNK):
        score[pl.ds(low, CHUNK), :] = jnp.zeros((CHUNK, rows), jnp.float32)

    def relu_pair(h):
        q0 = query_ref[:, pl.ds(pl.multiple_of(h * width, LANES), width)]
        q1 = query_ref[:, pl.ds(pl.multiple_of((h + 1) * width, LANES), width)]
        both = jnp.concatenate([q0, q1], 0)
        return lax.dot_general(panel[...], both, NT, preferred_element_type=jnp.float32)

    def score_step(i, carry):
        for u in range(unroll):
            h = (i * unroll + u) * 2
            value = relu_pair(h)
            g0 = gates[pl.ds(h, 1), :]
            g1 = gates[pl.ds(h + 1, 1), :]
            for low in range(0, keys, CHUNK):
                piece = jnp.maximum(value[low : low + CHUNK], 0.0)
                score[pl.ds(low, CHUNK), :] += piece[:, :rows] * g0 + piece[:, rows:] * g1
        return carry

    lax.fori_loop(0, heads // (2 * unroll), score_step, 0)

    first_row = idx_ref[0] * device_rows + block * rows
    panel_start = (idx_ref[0] - reach) * device_rows
    allowed = row_window(lens_ref, first_row, panel_start, keys, rows)
    peak = jnp.full((8, rows), floor_value, jnp.float32)
    for low in range(0, keys, CHUNK):
        piece = jnp.where(allowed(low, CHUNK), score[pl.ds(low, CHUNK), :] * factor, floor_value)
        score[pl.ds(low, CHUNK), :] = piece
        peak = jnp.maximum(peak, jnp.max(fold8(piece), 0))
    peak = jnp.max(peak, 0, keepdims=True)
    total = jnp.zeros((8, rows), jnp.float32)
    for low in range(0, keys, CHUNK):
        total = total + jnp.sum(fold8(jnp.exp(score[pl.ds(low, CHUNK), :] - peak)), 0)
    normal = peak + jnp.log(jnp.sum(total, 0, keepdims=True))
    spread = jnp.zeros((8, rows), jnp.float32)
    for low in range(0, keys, CHUNK):
        mask = allowed(low, CHUNK)
        log_model = jnp.where(mask, score[pl.ds(low, CHUNK), :] - normal, 0.0)
        target = target_ref[pl.ds(low, CHUNK), :]
        positive = target > 0
        log_target = jnp.log(jnp.where(positive, target, 1.0))
        spread = spread + jnp.sum(fold8(target * (log_target - log_model)), 0)
        score[pl.ds(low, CHUNK), :] = jnp.where(mask, jnp.exp(log_model), 0.0) - target
    div_ref[...] = jnp.sum(spread, 0, keepdims=True)

    def delta_step(i, carry):
        for u in range(unroll):
            h = (i * unroll + u) * 2
            value = relu_pair(h)
            sum0 = jnp.zeros((8, rows), jnp.float32)
            sum1 = jnp.zeros((8, rows), jnp.float32)
            for low in range(0, keys, CHUNK):
                piece = jnp.maximum(value[low : low + CHUNK], 0.0)
                weight_piece = score[pl.ds(low, CHUNK), :]
                sum0 = sum0 + jnp.sum(fold8(piece[:, :rows] * weight_piece), 0)
                sum1 = sum1 + jnp.sum(fold8(piece[:, rows:] * weight_piece), 0)
            delta[pl.ds(h, 1), :] = jnp.sum(sum0, 0, keepdims=True)
            delta[pl.ds(h + 1, 1), :] = jnp.sum(sum1, 0, keepdims=True)
        return carry

    lax.fori_loop(0, heads // (2 * unroll), delta_step, 0)

    gate_delta = (delta[...] * factor / device_rows).T
    zero = jnp.zeros_like(gate_delta)
    low_delta = jnp.concatenate([gate_delta, zero], 1).astype(jnp.bfloat16)
    high_delta = jnp.concatenate([zero, gate_delta], 1).astype(jnp.bfloat16)
    step = math.lcm(LANES, block_rows)
    for low in range(0, half, step):
        value = lax.dot_general(
            hidden_ref[:, low : low + step], low_delta, TN, preferred_element_type=jnp.float32
        ) + lax.dot_general(
            hidden_ref[:, half + low : half + low + step], high_delta, TN, preferred_element_type=jnp.float32
        )
        for i in range(step // block_rows):
            spot = reversed_bits(low // block_rows + i, bits)
            piece = value[i * block_rows : (i + 1) * block_rows]

            @pl.when(block == 0)
            def _():
                part_ref[spot] = piece

            @pl.when(block > 0)
            def _():
                part_ref[spot] += piece


def index_call(lengths, index, key_parts, target, hidden, weight, queries):
    reach = len(key_parts) - 1
    rows_all, cols = queries.shape
    width = key_parts[0].shape[1]
    rows = LANES
    keys = target.shape[0]
    heads = cols // width
    blocks, block_rows, lanes = weight.shape
    bits = blocks.bit_length() - 1
    depth = hidden.shape[1]
    return pl.pallas_call(
        functools.partial(index_kernel, reach, bits),
        out_shape=(
            jax.ShapeDtypeStruct((1, rows_all), jnp.float32),
            jax.ShapeDtypeStruct(weight.shape, jnp.float32),
        ),
        grid_spec=pltpu.PrefetchScalarGridSpec(
            num_scalar_prefetch=2,
            grid=(rows_all // rows,),
            in_specs=[pl.BlockSpec((rows_all, width), lambda i, *_: (0, 0))] * (reach + 1)
            + [
                pl.BlockSpec((keys, rows), lambda i, *_: (0, i)),
                pl.BlockSpec((rows, depth), lambda i, *_: (i, 0)),
                pl.BlockSpec(weight.shape, lambda i, *_: (0, 0, 0)),
                pl.BlockSpec((rows, cols), lambda i, *_: (i, 0)),
            ],
            out_specs=(
                pl.BlockSpec((1, rows), lambda i, *_: (0, i)),
                pl.BlockSpec(weight.shape, lambda i, *_: (0, 0, 0)),
            ),
            scratch_shapes=[
                pltpu.VMEM((keys, width), jnp.bfloat16),
                pltpu.VMEM((blocks * block_rows, lanes), jnp.bfloat16),
                pltpu.VMEM((heads, rows), jnp.float32),
                pltpu.VMEM((keys, rows), jnp.float32),
                pltpu.VMEM((heads, rows), jnp.float32),
            ],
        ),
        compiler_params=pltpu.CompilerParams(dimension_semantics=("arbitrary",)),
        cost_estimate=pl.CostEstimate(
            flops=4 * rows_all * cols * keys + 4 * rows_all * depth * heads,
            bytes_accessed=rows_all * (cols + depth) * 2 + 2 * depth * heads * 4,
            transcendentals=2 * rows_all * keys,
        ),
        name="index_terms",
    )(lengths, index, *key_parts, target, hidden, weight, queries)


def body(doc_lengths, hidden, gate_weight, target_query, latent_keys, index_query, index_keys):
    seq_count = lax.axis_size("seq")
    my_index = lax.axis_index("seq")
    row_count = hidden.shape[1]
    reach = min(LOOK, seq_count // 2)
    lengths = doc_lengths[0]
    index = my_index.reshape(1).astype(jnp.int32)
    steps = bit_steps()

    lat_parts = [shifted(latent_keys[0], "seq", d) for d in range(reach, 0, -1)] + [latent_keys[0]]
    key_parts = [shifted(index_keys[0], "seq", d) for d in range(reach, 0, -1)] + [index_keys[0]]

    axis, bit = steps[0]
    other = swap(gate_weight, axis, bit)
    mine_high = bit_of(axis, bit) == 1
    weight = jnp.where(
        mine_high, jnp.concatenate([other, gate_weight], 1), jnp.concatenate([gate_weight, other], 1)
    )[None]
    for axis, bit in steps[1:]:
        other = swap(weight, axis, bit)
        mine_high = bit_of(axis, bit) == 1
        weight = jnp.where(
            mine_high, jnp.concatenate([other, weight], 0), jnp.concatenate([weight, other], 0)
        )

    target = target_call(lengths, index, lat_parts, target_query[0])
    divergence, part = index_call(lengths, index, key_parts, target, hidden[0], weight, index_query[0])

    for axis, bit in reversed(steps[1:]):
        count = part.shape[0] // 2
        mine = bit_of(axis, bit)
        keep = lax.dynamic_slice_in_dim(part, mine * count, count, 0)
        send = lax.dynamic_slice_in_dim(part, (1 - mine) * count, count, 0)
        part = keep + swap(send, axis, bit)
    part = part[0]
    heads = part.shape[1] // 2
    axis, bit = steps[0]
    mine_high = bit_of(axis, bit) == 1
    low, high = part[:, :heads], part[:, heads:]
    keep = jnp.where(mine_high, high, low)
    send = jnp.where(mine_high, low, high)
    grad_gate = keep + swap(send, axis, bit)
    return divergence, grad_gate


def solution(mesh):
    in_specs = (
        P("grp", None),
        P("grp", "seq", None),
        P(("seq", "grp"), None),
        P("grp", "seq", None),
        P("grp", "seq", None),
        P("grp", "seq", None),
        P("grp", "seq", None),
    )
    out_specs = (P("grp", "seq"), P(("seq", "grp"), None))
    return jax.shard_map(body, mesh=mesh, in_specs=in_specs, out_specs=out_specs, check_vma=False)
```

time: 758 us -> 131 us (0.17); the launches traced: 749 us -> 130 us
  waiting for transfers between devices: 415 us -> 35.2 us
  local copies, waits for them, and re-layouts: 91.4 us -> 5.27 us
  matrix products: 69 us -> 0 us
  other arithmetic: 51.3 us -> 2.84 us
  Pallas kernels: 0 us -> 43.7 us
  loops' own time: 41.2 us -> 0 us
  blocking collectives: 40.9 us -> 0 us
  starting transfers between devices: 25.8 us -> 42.3 us
  between operations: 14.2 us -> 1.05 us
    unnamed x2 -> x0, waiting for transfers between devices: 412 us -> none
    dot_general x42 -> x0, matrix products: 69 us -> none  [the longest x8 19 us: first_pass(): jnp.einsum('brhc,bkc->brhk', queries, latent_tile, preferred_element_type...]
    pallas_call x0 -> x2, Pallas kernels: none -> 43.7 us  [the longest x1 28.8 us: target_call(): pl.pallas_call(functools.partial(target_kernel, reach), out_shape=jax.Sha...]
    another operation x17 -> x0, loops' own time: 41.2 us -> none  [the longest x1 39.1 us: piece_terms(): lax.map(one_batch, jnp.arange(batch_count, dtype=jnp.int32))]
    all_gather x1 -> x0, blocking collectives: 40.9 us -> none  [body(): full_gate = lax.all_gather(gate_weight, ('seq', 'grp'), axis=0, tiled=True)]
    ppermute x0 -> x10, waiting for transfers between devices: none -> 35.1 us  [swap(): lax.ppermute(block, axis, [(i, i ^ bit) for i in range(lax.axis_size(axis...]
    another operation x64 -> x0, local copies, waits for them, and re-layouts: 28.8 us -> none
    select_n x8 -> x0, local copies, waits for them, and re-layouts: 21.2 us -> none  [one_batch(): jnp.take(target_rows, chosen, axis=0)]
  transfers between devices with their start and end apart: 9 -> 18, of which waited for: 4 -> 8; matrix products, arithmetic and copies ran while one was open for 2% -> 2% of each run, Pallas kernels for 0% -> 22%
where the time goes in v1:
time: 131 us; the launch traced here: 130 us
  Pallas kernels  43.7 us (33%)
  starting transfers between devices  42.3 us (32%)
  waiting for transfers between devices  35.2 us (27%)
  local copies, waits for them, and re-layouts  5.27 us (4%)
  other arithmetic  2.84 us (2%)
    ppermute x10, waiting for transfers between devices, swap(): lax.ppermute(block, axis, [(i, i ^ bit) for i in range(lax.axis_size(axis...  35.1 us
    pallas_call x1, Pallas kernels, target_call(): pl.pallas_call(functools.partial(target_kernel, reach), out_shape=jax.Sha...  28.8 us
    ppermute x8, starting transfers between devices, shifted(): return lax.ppermute(block, axis, route)  23.2 us
    ppermute x10, starting transfers between devices, swap(): lax.ppermute(block, axis, [(i, i ^ bit) for i in range(lax.axis_size(axis...  19.1 us
    pallas_call x1, Pallas kernels, index_call(): pl.pallas_call(functools.partial(index_kernel, reach, bits), out_shape=(j...  14.8 us
    unnamed x25, local copies, waits for them, and re-layouts  3.81 us
  transfers between devices with their start and end apart: 18, of which 8 were waited for; matrix products, arithmetic and copies ran while one was open for 2% of the time, Pallas kernels for 22%

profile of v1, /device:TPU:0, one launch (start us, length us, event | category | flops | bytes accessed | tf_op | source)
XLA Modules:
  0.0 130.3 jit_solution(10686697732225166028)
XLA Ops:
  0.6 0.0 copy-start.6
  0.6 0.9 copy.10
  1.5 4.1 %collective-permute-start.8 = (bf16[224,64]{1,0:T(8,128)(2,1)S(1)}, bf16[224,64]{1,0:T(8,128)(2,1)S(1)}, u32[]{:S(2)}, u32[]{:S(2)}) collective-permute-start(bf16[224,64]{1,0:T(8,128)(2,1)S(1)} %copy.10), channel_id=1, source_target_pairs={{0,16},{4,20},{8,24},{12,28},{16,0},{20,4},{24,8},{28,12},{1,17},{... | collective-permute-start | bytes 86024 | tf_op jit(solution)/shard_map/ppermute | solution.py:39
  5.6 2.8 %collective-permute-done.8 = bf16[224,64]{1,0:T(8,128)(2,1)S(1)} collective-permute-done((bf16[224,64]{1,0:T(8,128)(2,1)S(1)}, bf16[224,64]{1,0:T(8,128)(2,1)S(1)}, u32[]{:S(2)}, u32[]{:S(2)}) %collective-permute-start.8) | collective-permute-done | bytes 28704 | tf_op jit(solution)/shard_map/ppermute | solution.py:39
  8.4 0.1 maximum_select_fusion.4
  8.5 1.4 %collective-permute-start.9 = (bf16[1,224,128]{2,1,0:T(8,128)(2,1)S(1)}, bf16[1,224,128]{2,1,0:T(8,128)(2,1)S(1)}, u32[]{:S(2)}, u32[]{:S(2)}) collective-permute-start(bf16[1,224,128]{2,1,0:T(8,128)(2,1)S(1)} %maximum_select_fusion.4), channel_id=1, source_target_pairs={{0,8},{4,12},{8,0},{12,4},{16,24},{20,28},{24,16},{28,20},{1,9},{5... | collective-permute-start | bytes 172040 | tf_op jit(solution)/shard_map/ppermute | solution.py:39
  9.9 2.9 %collective-permute-done.9 = bf16[1,224,128]{2,1,0:T(8,128)(2,1)S(1)} collective-permute-done((bf16[1,224,128]{2,1,0:T(8,128)(2,1)S(1)}, bf16[1,224,128]{2,1,0:T(8,128)(2,1)S(1)}, u32[]{:S(2)}, u32[]{:S(2)}) %collective-permute-start.9) | collective-permute-done | bytes 57376 | tf_op jit(solution)/shard_map/ppermute | solution.py:39
  12.8 1.8 %collective-permute-start.10 = (bf16[2,224,128]{2,1,0:T(8,128)(2,1)S(1)}, bf16[2,224,128]{2,1,0:T(8,128)(2,1)S(1)}, u32[]{:S(2)}, u32[]{:S(2)}) collective-permute-start(bf16[2,224,128]{2,1,0:T(8,128)(2,1)S(1)} %maximum_select_fusion.3), channel_id=1, source_target_pairs={{0,4},{4,0},{8,12},{12,8},{16,20},{20,16},{24,28},{28,24},{1,5},{5... | collective-permute-start | bytes 344072 | tf_op jit(solution)/shard_map/ppermute | solution.py:39
  14.6 3.1 %collective-permute-done.10 = bf16[2,224,128]{2,1,0:T(8,128)(2,1)S(1)} collective-permute-done((bf16[2,224,128]{2,1,0:T(8,128)(2,1)S(1)}, bf16[2,224,128]{2,1,0:T(8,128)(2,1)S(1)}, u32[]{:S(2)}, u32[]{:S(2)}) %collective-permute-start.10) | collective-permute-done | bytes 114720 | tf_op jit(solution)/shard_map/ppermute | solution.py:39
  17.7 1.8 %collective-permute-start.11 = (bf16[4,224,128]{2,1,0:T(8,128)(2,1)S(1)}, bf16[4,224,128]{2,1,0:T(8,128)(2,1)S(1)}, u32[]{:S(2)}, u32[]{:S(2)}) collective-permute-start(bf16[4,224,128]{2,1,0:T(8,128)(2,1)S(1)} %maximum_select_fusion.2), channel_id=1, source_target_pairs={{0,2},{1,3},{2,0},{3,1},{4,6},{5,7},{6,4},{7,5},{8,10},{9,11},{10,... | collective-permute-start | bytes 688136 | tf_op jit(solution)/shard_map/ppermute | solution.py:39
  19.4 1.1 copy.9
  20.5 0.0 copy-start.1
  20.5 4.2 %collective-permute-start.4 = (bf16[128,576]{1,0:T(8,128)(2,1)S(1)}, bf16[128,576]{1,0:T(8,128)(2,1)S(1)}, u32[]{:S(2)}, u32[]{:S(2)}) collective-permute-start(bf16[128,576]{1,0:T(8,128)(2,1)S(1)} %bitcast.12), channel_id=1, source_target_pairs={{0,16},{4,20},{8,24},{12,28},{1,17},{5,21},{9,25},{13,29},{2,18},{... | collective-permute-start | bytes 442376 | tf_op jit(solution)/shard_map/ppermute | solution.py:24
  24.7 4.9 %collective-permute-start.5 = (bf16[128,576]{1,0:T(8,128)(2,1)S(1)}, bf16[128,576]{1,0:T(8,128)(2,1)S(1)}, u32[]{:S(2)}, u32[]{:S(2)}) collective-permute-start(bf16[128,576]{1,0:T(8,128)(2,1)S(1)} %bitcast.13), channel_id=1, source_target_pairs={{0,12},{4,16},{8,20},{12,24},{16,28},{1,13},{5,17},{9,21},{13,25},... | collective-permute-start | bytes 442376 | tf_op jit(solution)/shard_map/ppermute | solution.py:24
  29.6 1.3 collective-permute-start.6
  30.9 3.1 %collective-permute-start.7 = (bf16[128,576]{1,0:T(8,128)(2,1)S(1)}, bf16[128,576]{1,0:T(8,128)(2,1)S(1)}, u32[]{:S(2)}, u32[]{:S(2)}) collective-permute-start(bf16[128,576]{1,0:T(8,128)(2,1)S(1)} %bitcast.15), channel_id=1, source_target_pairs={{0,4},{4,8},{8,12},{12,16},{16,20},{20,24},{24,28},{1,5},{5,9},{9,... | collective-permute-start | bytes 442376 | tf_op jit(solution)/shard_map/ppermute | solution.py:24
  34.0 0.0 collective-permute-done.11
  34.0 1.3 collective-permute-start
  35.3 0.1 maximum_select_fusion.1
  35.4 0.0 collective-permute-done.4.refs_0_
  35.4 0.0 copy-done.6
  35.4 0.0 copy-start.2
  35.5 2.2 %collective-permute-start.1 = (bf16[128,128]{1,0:T(8,128)(2,1)S(1)}, bf16[128,128]{1,0:T(8,128)(2,1)S(1)}, u32[]{:S(2)}, u32[]{:S(2)}) collective-permute-start(bf16[128,128]{1,0:T(8,128)(2,1)S(1)} %bitcast.23), channel_id=1, source_target_pairs={{0,12},{4,16},{8,20},{12,24},{16,28},{1,13},{5,17},{9,21},{13,25},... | collective-permute-start | bytes 98312 | tf_op jit(solution)/shard_map/ppermute | solution.py:24
  37.6 0.0 collective-permute-done.5.refs_1_
  37.6 0.0 copy-start.3
  37.7 1.3 collective-permute-start.2
  39.0 0.0 collective-permute-done.6.refs_2_
  39.0 0.0 copy-start.4
  39.0 5.0 %collective-permute-start.3 = (bf16[128,128]{1,0:T(8,128)(2,1)S(1)}, bf16[128,128]{1,0:T(8,128)(2,1)S(1)}, u32[]{:S(2)}, u32[]{:S(2)}) collective-permute-start(bf16[128,128]{1,0:T(8,128)(2,1)S(1)} %bitcast.25), channel_id=1, source_target_pairs={{0,4},{4,8},{8,12},{12,16},{16,20},{20,24},{24,28},{1,5},{5,9},{9,... | collective-permute-start | bytes 98312 | tf_op jit(solution)/shard_map/ppermute | solution.py:24
  44.0 0.0 collective-permute-done.7.refs_3_
  44.0 0.0 copy-start.5
  44.0 0.1 collective-permute-start.12
  44.1 0.0 copy-done.1
  44.1 0.0 copy-done.2
  44.1 0.0 copy-done.3
  44.1 0.5 copy-done.5
  44.7 28.8 %target_terms.1.refs_5_ = f32[640,128]{1,0:T(8,128)} custom-call(s32[4]{0:T(128)} %bitcast.26, s32[1]{0:T(128)} %bitcast.1.idx_ref, bf16[128,576]{1,0:T(8,128)(2,1)} %copy-done.2, bf16[128,576]{1,0:T(8,128)(2,1)} %copy-done.3, bf16[128,576]{1,0:T(8,128)(2,1)} %copy-done.4, bf16[128,576]{1,0:T(8,128)(2,1)} %copy-done.5, bf16[128,576]{1,0:T(8,128)(2,1)} %bitcast.16, ...), custom_call_target="tpu_custom_call" | custom-call | flops 6039797760 | bytes 9437184 | tf_op jit(solution)/shard_map/target_terms/pallas_call | solution.py:168
  73.5 0.0 collective-permute-done.12
  73.5 1.1 maximum_select_fusion.refs_7_
  74.6 0.0 collective-permute-done.refs_0_
  74.6 0.0 collective-permute-done.1.refs_1_
  74.6 0.0 copy-start.8
  74.6 0.0 collective-permute-done.2.refs_2_
  74.7 0.0 collective-permute-done.3.refs_3_
  74.7 0.6 copy-done.7
  75.2 0.0 copy-done.9
  75.3 0.0 copy-done.10
  75.3 14.8 %index_terms.1 = (f32[1,128]{1,0:T(1,128)}, f32[16,224,128]{2,1,0:T(8,128)}) custom-call(s32[4]{0:T(128)} %bitcast.27, s32[1]{0:T(128)} %bitcast.1.idx_ref, bf16[128,128]{1,0:T(8,128)(2,1)} %copy-done.7, bf16[128,128]{1,0:T(8,128)(2,1)} %copy-done.8, bf16[128,128]{1,0:T(8,128)(2,1)} %copy-done.9, bf16[128,128]{1,0:T(8,128)(2,1)} %copy-done.10, ...), custom_call_target="tpu_custom_call" | custom-call | flops 2919235584 | bytes 7602176 | tf_op jit(solution)/shard_map/index_terms/pallas_call | solution.py:318
  90.1 1.4 %constant_dynamic-slice_fusion.3 = f32[8,224,128]{2,1,0:T(8,128)S(1)} fusion(f32[16,224,128]{2,1,0:T(8,128)} %get-tuple-element.5, s32[]{:T(128)S(6)} %select_n.153), kind=kLoop, calls=%fused_computation.14 | loop fusion | bytes 1835012 | tf_op jit(solution)/shard_map/dynamic_slice | solution.py:388
  91.5 0.1 collective-permute-start.13
  91.6 2.6 %collective-permute-done.13 = f32[8,224,128]{2,1,0:T(8,128)} collective-permute-done((f32[8,224,128]{2,1,0:T(8,128)S(1)}, f32[8,224,128]{2,1,0:T(8,128)}, u32[]{:S(2)}, u32[]{:S(2)}) %collective-permute-start.13) | collective-permute-done | bytes 917536 | tf_op jit(solution)/shard_map/ppermute | solution.py:39
  94.2 0.0 copy-done
  94.2 1.3 dynamic-slice_add_fusion
  95.5 0.6 collective-permute-start.14
  96.1 12.0 %collective-permute-done.14 = f32[4,224,128]{2,1,0:T(8,128)S(1)} collective-permute-done((f32[4,224,128]{2,1,0:T(8,128)S(1)}, f32[4,224,128]{2,1,0:T(8,128)S(1)}, u32[]{:S(2)}, u32[]{:S(2)}) %collective-permute-start.14) | collective-permute-done | bytes 458784 | tf_op jit(solution)/shard_map/ppermute | solution.py:39
  108.2 2.6 %collective-permute-start.15 = (f32[2,224,128]{2,1,0:T(8,128)S(1)}, f32[2,224,128]{2,1,0:T(8,128)S(1)}, u32[]{:S(2)}, u32[]{:S(2)}) collective-permute-start(f32[2,224,128]{2,1,0:T(8,128)S(1)} %constant_dynamic-slice_fusion.1), channel_id=1, source_target_pairs={{0,4},{4,0},{8,12},{12,8},{16,20},{20,16},{24,28},{28,24},{1,5},{5... | collective-permute-start | bytes 688136 | tf_op jit(solution)/shard_map/ppermute | solution.py:39
  110.8 5.0 %collective-permute-done.15 = f32[2,224,128]{2,1,0:T(8,128)S(1)} collective-permute-done((f32[2,224,128]{2,1,0:T(8,128)S(1)}, f32[2,224,128]{2,1,0:T(8,128)S(1)}, u32[]{:S(2)}, u32[]{:S(2)}) %collective-permute-start.15) | collective-permute-done | bytes 229408 | tf_op jit(solution)/shard_map/ppermute | solution.py:39
  115.9 3.0 %collective-permute-start.16 = (f32[1,224,128]{2,1,0:T(8,128)S(1)}, f32[1,224,128]{2,1,0:T(8,128)S(1)}, u32[]{:S(2)}, u32[]{:S(2)}) collective-permute-start(f32[1,224,128]{2,1,0:T(8,128)S(1)} %constant_dynamic-slice_fusion), channel_id=1, source_target_pairs={{0,8},{4,12},{8,0},{12,4},{16,24},{20,28},{24,16},{28,20},{1,9},{5... | collective-permute-start | bytes 344072 | tf_op jit(solution)/shard_map/ppermute | solution.py:39
  118.9 2.8 %collective-permute-done.16 = f32[1,224,128]{2,1,0:T(8,128)S(1)} collective-permute-done((f32[1,224,128]{2,1,0:T(8,128)S(1)}, f32[1,224,128]{2,1,0:T(8,128)S(1)}, u32[]{:S(2)}, u32[]{:S(2)}) %collective-permute-start.16) | collective-permute-done | bytes 114720 | tf_op jit(solution)/shard_map/ppermute | solution.py:39
  121.7 0.1 slice_select_fusion
  121.8 3.7 %collective-permute-start.17 = (f32[224,64]{1,0:T(8,128)S(1)}, f32[224,64]{1,0:T(8,128)S(1)}, u32[]{:S(2)}, u32[]{:S(2)}) collective-permute-start(f32[224,64]{1,0:T(8,128)S(1)} %slice_select_fusion), channel_id=1, source_target_pairs={{0,16},{4,20},{8,24},{12,28},{16,0},{20,4},{24,8},{28,12},{1,17},{... | collective-permute-start | bytes 172040 | tf_op jit(solution)/shard_map/ppermute | solution.py:39
  125.5 4.0 %collective-permute-done.17 = f32[224,64]{1,0:T(8,128)S(1)} collective-permute-done((f32[224,64]{1,0:T(8,128)S(1)}, f32[224,64]{1,0:T(8,128)S(1)}, u32[]{:S(2)}, u32[]{:S(2)}) %collective-permute-start.17) | collective-permute-done | bytes 57376 | tf_op jit(solution)/shard_map/ppermute | solution.py:39
  129.5 0.1 select_add_fusion
  129.6 0.7 copy.12
  (14 shorter events, 0.2 us)
Async XLA Ops:
  0.6 34.8 %copy-start.6 = (bf16[1,128,128]{2,1,0:T(8,128)(2,1)S(1)}, bf16[1,128,128]{2,1,0:T(8,128)(2,1)}, u32[]{:S(2)}) copy-start(bf16[1,128,128]{2,1,0:T(8,128)(2,1)} %param.13) | copy-start | bytes 98308
  1.5 6.9 %collective-permute-start.8 = (bf16[224,64]{1,0:T(8,128)(2,1)S(1)}, bf16[224,64]{1,0:T(8,128)(2,1)S(1)}, u32[]{:S(2)}, u32[]{:S(2)}) collective-permute-start(bf16[224,64]{1,0:T(8,128)(2,1)S(1)} %copy.10), channel_id=1, source_target_pairs={{0,16},{4,20},{8,24},{12,28},{16,0},{20,4},{24,8},{28,12},{1,17},{... | collective-permute-start | bytes 86024 | tf_op jit(solution)/shard_map/ppermute | solution.py:39
  8.5 4.2 %collective-permute-start.9 = (bf16[1,224,128]{2,1,0:T(8,128)(2,1)S(1)}, bf16[1,224,128]{2,1,0:T(8,128)(2,1)S(1)}, u32[]{:S(2)}, u32[]{:S(2)}) collective-permute-start(bf16[1,224,128]{2,1,0:T(8,128)(2,1)S(1)} %maximum_select_fusion.4), channel_id=1, source_target_pairs={{0,8},{4,12},{8,0},{12,4},{16,24},{20,28},{24,16},{28,20},{1,9},{5... | collective-permute-start | bytes 172040 | tf_op jit(solution)/shard_map/ppermute | solution.py:39
  12.8 4.9 %collective-permute-start.10 = (bf16[2,224,128]{2,1,0:T(8,128)(2,1)S(1)}, bf16[2,224,128]{2,1,0:T(8,128)(2,1)S(1)}, u32[]{:S(2)}, u32[]{:S(2)}) collective-permute-start(bf16[2,224,128]{2,1,0:T(8,128)(2,1)S(1)} %maximum_select_fusion.3), channel_id=1, source_target_pairs={{0,4},{4,0},{8,12},{12,8},{16,20},{20,16},{24,28},{28,24},{1,5},{5... | collective-permute-start | bytes 344072 | tf_op jit(solution)/shard_map/ppermute | solution.py:39
  17.7 16.4 %collective-permute-start.11 = (bf16[4,224,128]{2,1,0:T(8,128)(2,1)S(1)}, bf16[4,224,128]{2,1,0:T(8,128)(2,1)S(1)}, u32[]{:S(2)}, u32[]{:S(2)}) collective-permute-start(bf16[4,224,128]{2,1,0:T(8,128)(2,1)S(1)} %maximum_select_fusion.2), channel_id=1, source_target_pairs={{0,2},{1,3},{2,0},{3,1},{4,6},{5,7},{6,4},{7,5},{8,10},{9,11},{10,... | collective-permute-start | bytes 688136 | tf_op jit(solution)/shard_map/ppermute | solution.py:39
  20.5 23.6 %copy-start.1 = (bf16[1,128,576]{2,1,0:T(8,128)(2,1)}, bf16[1,128,576]{2,1,0:T(8,128)(2,1)S(1)}, u32[]{:S(2)}) copy-start(bf16[1,128,576]{2,1,0:T(8,128)(2,1)S(1)} %copy.9) | copy-start | bytes 442372
  20.5 14.9 %collective-permute-start.4 = (bf16[128,576]{1,0:T(8,128)(2,1)S(1)}, bf16[128,576]{1,0:T(8,128)(2,1)S(1)}, u32[]{:S(2)}, u32[]{:S(2)}) collective-permute-start(bf16[128,576]{1,0:T(8,128)(2,1)S(1)} %bitcast.12), channel_id=1, source_target_pairs={{0,16},{4,20},{8,24},{12,28},{1,17},{5,21},{9,25},{13,29},{2,18},{... | collective-permute-start | bytes 442376 | tf_op jit(solution)/shard_map/ppermute | solution.py:24
  24.7 13.0 %collective-permute-start.5 = (bf16[128,576]{1,0:T(8,128)(2,1)S(1)}, bf16[128,576]{1,0:T(8,128)(2,1)S(1)}, u32[]{:S(2)}, u32[]{:S(2)}) collective-permute-start(bf16[128,576]{1,0:T(8,128)(2,1)S(1)} %bitcast.13), channel_id=1, source_target_pairs={{0,12},{4,16},{8,20},{12,24},{16,28},{1,13},{5,17},{9,21},{13,25},... | collective-permute-start | bytes 442376 | tf_op jit(solution)/shard_map/ppermute | solution.py:24
  29.6 9.4 %collective-permute-start.6 = (bf16[128,576]{1,0:T(8,128)(2,1)S(1)}, bf16[128,576]{1,0:T(8,128)(2,1)S(1)}, u32[]{:S(2)}, u32[]{:S(2)}) collective-permute-start(bf16[128,576]{1,0:T(8,128)(2,1)S(1)} %bitcast.14), channel_id=1, source_target_pairs={{0,8},{4,12},{8,16},{12,20},{16,24},{20,28},{1,9},{5,13},{9,17},{1... | collective-permute-start | bytes 442376 | tf_op jit(solution)/shard_map/ppermute | solution.py:24
  30.9 13.1 %collective-permute-start.7 = (bf16[128,576]{1,0:T(8,128)(2,1)S(1)}, bf16[128,576]{1,0:T(8,128)(2,1)S(1)}, u32[]{:S(2)}, u32[]{:S(2)}) collective-permute-start(bf16[128,576]{1,0:T(8,128)(2,1)S(1)} %bitcast.15), channel_id=1, source_target_pairs={{0,4},{4,8},{8,12},{12,16},{16,20},{20,24},{24,28},{1,5},{5,9},{9,... | collective-permute-start | bytes 442376 | tf_op jit(solution)/shard_map/ppermute | solution.py:24
  34.0 40.6 %collective-permute-start = (bf16[128,128]{1,0:T(8,128)(2,1)}, bf16[128,128]{1,0:T(8,128)(2,1)S(1)}, u32[]{:S(2)}, u32[]{:S(2)}) collective-permute-start(bf16[128,128]{1,0:T(8,128)(2,1)} %bitcast.21), channel_id=1, source_target_pairs={{0,16},{4,20},{8,24},{12,28},{1,17},{5,21},{9,25},{13,29},{2,18},{... | collective-permute-start | bytes 98312 | tf_op jit(solution)/shard_map/ppermute | solution.py:24
  35.4 8.7 %copy-start.2 = (bf16[128,576]{1,0:T(8,128)(2,1)}, bf16[128,576]{1,0:T(8,128)(2,1)S(1)}, u32[]{:S(2)}) copy-start(bf16[128,576]{1,0:T(8,128)(2,1)S(1)} %collective-permute-done.4.refs_0_) | copy-start | bytes 442372
  35.5 39.2 %collective-permute-start.1 = (bf16[128,128]{1,0:T(8,128)(2,1)S(1)}, bf16[128,128]{1,0:T(8,128)(2,1)S(1)}, u32[]{:S(2)}, u32[]{:S(2)}) collective-permute-start(bf16[128,128]{1,0:T(8,128)(2,1)S(1)} %bitcast.23), channel_id=1, source_target_pairs={{0,12},{4,16},{8,20},{12,24},{16,28},{1,13},{5,17},{9,21},{13,25},... | collective-permute-start | bytes 98312 | tf_op jit(solution)/shard_map/ppermute | solution.py:24
  37.6 6.5 %copy-start.3 = (bf16[128,576]{1,0:T(8,128)(2,1)}, bf16[128,576]{1,0:T(8,128)(2,1)S(1)}, u32[]{:S(2)}) copy-start(bf16[128,576]{1,0:T(8,128)(2,1)S(1)} %collective-permute-done.5.refs_1_) | copy-start | bytes 442372
  37.7 37.0 %collective-permute-start.2 = (bf16[128,128]{1,0:T(8,128)(2,1)S(1)}, bf16[128,128]{1,0:T(8,128)(2,1)S(1)}, u32[]{:S(2)}, u32[]{:S(2)}) collective-permute-start(bf16[128,128]{1,0:T(8,128)(2,1)S(1)} %bitcast.24), channel_id=1, source_target_pairs={{0,8},{4,12},{8,16},{12,20},{16,24},{20,28},{1,9},{5,13},{9,17},{1... | collective-permute-start | bytes 98312 | tf_op jit(solution)/shard_map/ppermute | solution.py:24
  39.0 5.2 %copy-start.4 = (bf16[128,576]{1,0:T(8,128)(2,1)}, bf16[128,576]{1,0:T(8,128)(2,1)S(1)}, u32[]{:S(2)}) copy-start(bf16[128,576]{1,0:T(8,128)(2,1)S(1)} %collective-permute-done.6.refs_2_) | copy-start | bytes 442372
  39.0 35.7 %collective-permute-start.3 = (bf16[128,128]{1,0:T(8,128)(2,1)S(1)}, bf16[128,128]{1,0:T(8,128)(2,1)S(1)}, u32[]{:S(2)}, u32[]{:S(2)}) collective-permute-start(bf16[128,128]{1,0:T(8,128)(2,1)S(1)} %bitcast.25), channel_id=1, source_target_pairs={{0,4},{4,8},{8,12},{12,16},{16,20},{20,24},{24,28},{1,5},{5,9},{9,... | collective-permute-start | bytes 98312 | tf_op jit(solution)/shard_map/ppermute | solution.py:24
  44.0 0.7 copy-start.5
  44.0 29.5 %collective-permute-start.12 = (bf16[8,224,128]{2,1,0:T(8,128)(2,1)S(1)}, bf16[8,224,128]{2,1,0:T(8,128)(2,1)S(1)}, u32[]{:S(2)}, u32[]{:S(2)}) collective-permute-start(bf16[8,224,128]{2,1,0:T(8,128)(2,1)S(1)} %maximum_select_fusion.1), channel_id=1, source_target_pairs={{0,1},{1,0},{2,3},{3,2},{4,5},{5,4},{6,7},{7,6},{8,9},{9,8},{10,11... | collective-permute-start | bytes 1376264 | tf_op jit(solution)/shard_map/ppermute | solution.py:39
  74.6 0.6 copy-start.7
  74.6 0.6 copy-start.8
  74.7 0.6 copy-start.9
  74.7 0.6 copy-start.10
  90.1 4.1 %copy-start = (f32[16,224,128]{2,1,0:T(8,128)S(1)}, f32[16,224,128]{2,1,0:T(8,128)}, u32[]{:S(2)}) copy-start(f32[16,224,128]{2,1,0:T(8,128)} %get-tuple-element.5) | copy-start | bytes 5505028
  91.5 2.7 %collective-permute-start.13 = (f32[8,224,128]{2,1,0:T(8,128)S(1)}, f32[8,224,128]{2,1,0:T(8,128)}, u32[]{:S(2)}, u32[]{:S(2)}) collective-permute-start(f32[8,224,128]{2,1,0:T(8,128)S(1)} %constant_dynamic-slice_fusion.3), channel_id=1, source_target_pairs={{0,1},{1,0},{2,3},{3,2},{4,5},{5,4},{6,7},{7,6},{8,9},{9,8},{10,11... | collective-permute-start | bytes 2752520 | tf_op jit(solution)/shard_map/ppermute | solution.py:39
  95.5 12.6 %collective-permute-start.14 = (f32[4,224,128]{2,1,0:T(8,128)S(1)}, f32[4,224,128]{2,1,0:T(8,128)S(1)}, u32[]{:S(2)}, u32[]{:S(2)}) collective-permute-start(f32[4,224,128]{2,1,0:T(8,128)S(1)} %constant_dynamic-slice_fusion.2), channel_id=1, source_target_pairs={{0,2},{1,3},{2,0},{3,1},{4,6},{5,7},{6,4},{7,5},{8,10},{9,11},{10,... | collective-permute-start | bytes 1376264 | tf_op jit(solution)/shard_map/ppermute | solution.py:39
  108.2 7.7 %collective-permute-start.15 = (f32[2,224,128]{2,1,0:T(8,128)S(1)}, f32[2,224,128]{2,1,0:T(8,128)S(1)}, u32[]{:S(2)}, u32[]{:S(2)}) collective-permute-start(f32[2,224,128]{2,1,0:T(8,128)S(1)} %constant_dynamic-slice_fusion.1), channel_id=1, source_target_pairs={{0,4},{4,0},{8,12},{12,8},{16,20},{20,16},{24,28},{28,24},{1,5},{5... | collective-permute-start | bytes 688136 | tf_op jit(solution)/shard_map/ppermute | solution.py:39
  115.9 5.8 %collective-permute-start.16 = (f32[1,224,128]{2,1,0:T(8,128)S(1)}, f32[1,224,128]{2,1,0:T(8,128)S(1)}, u32[]{:S(2)}, u32[]{:S(2)}) collective-permute-start(f32[1,224,128]{2,1,0:T(8,128)S(1)} %constant_dynamic-slice_fusion), channel_id=1, source_target_pairs={{0,8},{4,12},{8,0},{12,4},{16,24},{20,28},{24,16},{28,20},{1,9},{5... | collective-permute-start | bytes 344072 | tf_op jit(solution)/shard_map/ppermute | solution.py:39
  121.8 7.7 %collective-permute-start.17 = (f32[224,64]{1,0:T(8,128)S(1)}, f32[224,64]{1,0:T(8,128)S(1)}, u32[]{:S(2)}, u32[]{:S(2)}) collective-permute-start(f32[224,64]{1,0:T(8,128)S(1)} %slice_select_fusion), channel_id=1, source_target_pairs={{0,16},{4,20},{8,24},{12,28},{16,0},{20,4},{24,8},{28,12},{1,17},{... | collective-permute-start | bytes 172040 | tf_op jit(solution)/shard_map/ppermute | solution.py:39
